TPU v7x, 256 devices: a whole 4x4x8 slice. The times are simulated.
256 devices in a mesh: dish: 8 (over y_hi, x), chan: 32 (over y_lo, z, core).
Axes of the slice: x: 4, y: 4 (y_hi: 2, y_lo: 2; y = y_hi * 2 + y_lo), z: 8, core: 2. Of those that a mesh axis runs over, the one named last changes fastest.
Arguments:
- voltages: bfloat16 [2, 64, 4096, 512], P(None, 'dish', 'chan'), may hold values from -150 to 150
- beam_weights: bfloat16 [2, 4096, 64, 1024], P(None, ('chan', 'dish')), may hold values from -0.5 to 0.5
- flags: int32 [4096], P('chan'), may hold values 0 or 1
- sk_bins: int32 [4096], P('chan'), may hold values from 1 to 8
- bin_of_sample: int32 [512], replicated, may hold values from 0 to 63, never falling along the last dimension, each value on 1 to 16 neighbouring positions
Outputs:
- beam_power: bfloat16 [4096, 65536], P(None, ('dish', 'chan'))
Inputs may be any that keep to these rules, and one draw needn't show every extreme that they name: `bin_of_sample`: never falls; each of the 64 bins holds 1 to 16 samples.
All inputs are finite; a program needn't handle non-finite values. No bound on the sum of `flags` on one device may be relied on, other than what follows from the above.
Results may differ from a plain program's by a relative error of at most 0.006.
Values may be sent and summed in bfloat16 or wider, within the bound.
No kernel may reach another device: no remote copies, remote signals or barrier semaphores. Data moves between devices by JAX's collectives and lax.ppermute only.
A program may use at most 64 MiB of HBM per device.

v0:
```python
import jax
import jax.numpy as jnp
from jax import lax
from jax.sharding import PartitionSpec as P

TBINS = 64


def cut_along(value, dim, length):
    before, after = (value.shape[:dim], value.shape[dim + 1 :])
    return jnp.moveaxis(value.reshape(*before, length, -1, *after), dim, 0)


def piece_ends(length, count):
    unit = 8 if length >= 8 * count else 1
    return [length // unit * k // count * unit for k in range(1, count)]


def laid_out(tiles, dim):
    tiles = jnp.moveaxis(tiles, 0, dim)
    shape = tiles.shape
    return tiles.reshape(*shape[:dim], shape[dim] * shape[dim + 1], *shape[dim + 2 :])


def several_exchanges(value, axis, pieces, split_dim, concat_dim):
    tiles = cut_along(value, split_dim, lax.axis_size(axis))
    split_at = max(range(1, max(2, tiles.ndim - 1)), key=lambda d: tiles.shape[d])
    gathered = []
    for section in jnp.split(tiles, piece_ends(tiles.shape[split_at], pieces), axis=split_at):
        if section.size:
            gathered.append(lax.all_to_all(section, axis, split_axis=0, concat_axis=0, tiled=True))
    return laid_out(jnp.concatenate(gathered, axis=split_at), concat_dim)


def exchange_both(value, axis, axes, splits, concats):
    sizes = [lax.axis_size(a) for a in axes]
    tiles = cut_along(value, splits[0], sizes[0])
    tiles = jnp.moveaxis(cut_along(tiles, splits[1] + 1, sizes[1]), 0, 1)
    inside = tiles.shape[2:]
    tiles = tiles.reshape(-1, *inside)
    tiles = lax.all_to_all(tiles, axis, split_axis=0, concat_axis=0, tiled=True)
    tiles = laid_out(tiles.reshape(*sizes, *inside), concats[0] + 1)
    return laid_out(tiles, concats[1])


def kurtosis_scale(first_sum, second_sum, samples, flags, sk_bins):
    widths = 0.05 * sk_bins.astype(jnp.float32)
    mean_one = first_sum / samples
    mean_two = second_sum / samples
    ratio = mean_two / (mean_one * mean_one + 1e-06)
    kurtosis = (samples + 1.0) / (samples - 1.0) * (ratio - 1.0)
    excess = kurtosis - 1.0
    return flags.astype(jnp.float32) * widths / (widths + excess * excess)


def moment_sums(volts):
    floats = volts.astype(jnp.float32)
    powers = floats[0] * floats[0] + floats[1] * floats[1]
    return (jnp.sum(powers, axis=(0, 2)), jnp.sum(powers * powers, axis=(0, 2)))


def apply_scale(volts, scaling):
    return (volts.astype(jnp.float32) * scaling[None, None, :, None]).astype(jnp.bfloat16)


def channel_average(volts, weights, onehot, counts):
    stacked_v = jnp.concatenate([volts[0], volts[1]], axis=0)
    real_rows = jnp.concatenate([weights[0], -weights[1]], axis=0)
    imag_rows = jnp.concatenate([weights[1], weights[0]], axis=0)
    stacked_w = jnp.concatenate([real_rows, imag_rows], axis=1)
    beam_volts = jnp.dot(stacked_w.T, stacked_v, preferred_element_type=jnp.float32)
    half = weights.shape[2]
    real_part = beam_volts[:half]
    imag_part = beam_volts[half:]
    powers = real_part * real_part + imag_part * imag_part
    upper = powers.astype(jnp.bfloat16)
    lower = (powers - upper.astype(jnp.float32)).astype(jnp.bfloat16)
    summed = jnp.dot(upper, onehot, preferred_element_type=jnp.float32) + jnp.dot(
        lower, onehot, preferred_element_type=jnp.float32
    )
    return (summed / counts[None, :]).astype(jnp.bfloat16)


def body(voltages, beam_weights, flags, sk_bins, bin_of_sample):
    dish_count = lax.axis_size("dish")
    chan_count = lax.axis_size("chan")
    samples = float(voltages.shape[1] * dish_count * voltages.shape[3])
    arrived = several_exchanges(voltages, "dish", 2, 2, 1)
    first_sum, second_sum = moment_sums(arrived)
    chan_here = arrived.shape[2]
    offset = lax.axis_index("dish") * chan_here
    local_flags = lax.dynamic_slice_in_dim(flags, offset, chan_here)
    local_bins = lax.dynamic_slice_in_dim(sk_bins, offset, chan_here)
    scaling = kurtosis_scale(first_sum, second_sum, samples, local_flags, local_bins)
    turned = apply_scale(arrived, scaling)
    chan_here = turned.shape[2]
    matches = bin_of_sample[:, None] == jnp.arange(TBINS, dtype=jnp.int32)[None, :]
    onehot = matches.astype(jnp.bfloat16)
    counts = jnp.sum(matches.astype(jnp.float32), axis=0)

    def one_channel(index):
        volts = lax.dynamic_index_in_dim(turned, index, 2, keepdims=False)
        weights = lax.dynamic_index_in_dim(beam_weights, index, 1, keepdims=False)
        return channel_average(volts, weights, onehot, counts)

    averaged = lax.map(one_channel, jnp.arange(chan_here, dtype=jnp.int32))
    beam_total = beam_weights.shape[3]
    per_owner = beam_total // (dish_count * chan_count)
    blocks = averaged.reshape(1, 1, chan_here, dish_count, chan_count, per_owner * TBINS)
    moved = exchange_both(blocks, ("dish", "chan"), ("dish", "chan"), (3, 4), (1, 0))
    return moved.reshape(chan_count * dish_count * chan_here, per_owner * TBINS)


def solution(mesh):
    in_specs = (
        P(None, "dish", "chan", None),
        P(None, ("chan", "dish"), None, None),
        P("chan"),
        P("chan"),
        P(),
    )
    out_specs = P(None, ("dish", "chan"))
    return jax.shard_map(body, mesh=mesh, in_specs=in_specs, out_specs=out_specs, check_vma=False)
```

profile of v0, /device:TPU:1, one launch (start us, length us, event | category | flops | bytes accessed | tf_op | source)
XLA Modules:
  0.0 238.7 jit_solution(9565417412287759718)
XLA Ops:
  0.0 1.7 fusion.33
  1.7 1.5 copy.26
  3.3 7.5 %all-to-all-start = ((bf16[8,2,8,8,512]{4,2,3,1,0:T(8,128)(2,1)}), bf16[8,2,8,8,512]{4,2,3,1,0:T(8,128)(2,1)S(1)}, u32[]{:S(2)}, u32[]{:S(2)}) async-start(bf16[8,2,8,8,512]{4,2,3,1,0:T(8,128)(2,1)} %copy.26), calls=%async_computation | async-start | bytes 2097152 | tf_op jit(solution)/shard_map/all_to_all | solution.py:31
  10.8 1.5 copy.27
  12.3 15.8 %all-to-all-done = bf16[8,2,8,8,512]{4,2,3,1,0:T(8,128)(2,1)S(1)} async-done(((bf16[8,2,8,8,512]{4,2,3,1,0:T(8,128)(2,1)}), bf16[8,2,8,8,512]{4,2,3,1,0:T(8,128)(2,1)S(1)}, u32[]{:S(2)}, u32[]{:S(2)}) %all-to-all-start) | async-done | bytes 1048608 | tf_op jit(solution)/shard_map/all_to_all | solution.py:31
  28.1 3.6 %all-to-all-start.1 = ((bf16[8,2,8,8,512]{4,2,3,1,0:T(8,128)(2,1)}), bf16[8,2,8,8,512]{4,2,3,1,0:T(8,128)(2,1)S(1)}, u32[]{:S(2)}, u32[]{:S(2)}) async-start(bf16[8,2,8,8,512]{4,2,3,1,0:T(8,128)(2,1)} %copy.27), calls=%async_computation.1 | async-start | bytes 2097152 | tf_op jit(solution)/shard_map/all_to_all | solution.py:31
  32.2 16.8 %all-to-all-done.1 = bf16[8,2,8,8,512]{4,2,3,1,0:T(8,128)(2,1)S(1)} async-done(((bf16[8,2,8,8,512]{4,2,3,1,0:T(8,128)(2,1)}), bf16[8,2,8,8,512]{4,2,3,1,0:T(8,128)(2,1)S(1)}, u32[]{:S(2)}, u32[]{:S(2)}) %all-to-all-start.1) | async-done | bytes 1048608 | tf_op jit(solution)/shard_map/all_to_all | solution.py:31
  53.3 108.5 %while.11 = (s32[]{:T(128)}, bf16[16,1024,64]{1,2,0:T(8,128)(2,1)}, s32[16]{0:T(128)S(1)}, bf16[2,16,64,1024]{3,2,1,0:T(8,128)(2,1)}, bf16[2,64,16,512]{3,1,2,0:...) while((s32[]{:T(128)}, bf16[16,1024,64]{1,2,0:T(8,128)(2,1)}, ...), condition=%wide.region_4.5_spmd.clone, body=%wide.region_3.4_spmd.clone.sunk | while | flops 411172864 | bytes 14685115 | solution.py:106
  58.9 1.2 fusion.51
  65.7 1.2 fusion.51
  72.5 1.2 fusion.51
  92.8 1.2 fusion.51
  99.6 1.2 fusion.51
  106.4 1.2 fusion.51
  113.2 1.2 fusion.51
  133.5 1.2 fusion.51
  140.3 1.2 fusion.51
  147.1 1.2 fusion.51
  153.8 1.2 fusion.51
  160.6 1.2 fusion.51
  161.8 4.8 %copy.31 = bf16[16,1024,64]{2,1,0:T(8,128)(2,1)} copy(bf16[16,1024,64]{1,2,0:T(8,128)(2,1)} %get-tuple-element.42) | data formatting | bytes 4194304 | tf_op jit(solution)/shard_map/while | solution.py:106
  166.6 5.5 %reshape_reshape.3 = bf16[1,1,16,8,1,32,256]{6,5,3,2,4,1,0:T(8,128)(2,1)S(1)} reshape(bf16[16,1024,64]{2,1,0:T(8,128)(2,1)} %copy.31) | data formatting | bytes 4194304 | tf_op jit(solution)/shard_map/reshape;reshape | solution.py:11
  173.3 63.8 %all_to_all.15 = bf16[256,1,1,16,1,1,256]{6,3,5,4,2,1,0:T(8,128)(2,1)S(1)} all-to-all(bf16[256,1,1,16,1,1,256]{6,3,5,4,2,1,0:T(8,128)(2,1)S(1)} %copy.32), channel_id=1, replica_groups=mesh['dish'=8,'chan'=32] {'dish','chan'}, dimensions={0} | all-to-all | bytes 4194304 | tf_op jit(solution)/shard_map/all_to_all | solution.py:41
  237.1 1.6 copy.33
  (117 shorter events, 70.0 us)
Async XLA Ops:
  3.3 24.8 %all-to-all-start = ((bf16[8,2,8,8,512]{4,2,3,1,0:T(8,128)(2,1)}), bf16[8,2,8,8,512]{4,2,3,1,0:T(8,128)(2,1)S(1)}, u32[]{:S(2)}, u32[]{:S(2)}) async-start(bf16[8,2,8,8,512]{4,2,3,1,0:T(8,128)(2,1)} %copy.26), calls=%async_computation | async-start | bytes 2097152 | tf_op jit(solution)/shard_map/all_to_all | solution.py:31
  10.8 21.0 %copy-start = (s32[512]{0:T(512)S(1)}, s32[512]{0:T(512)}, u32[]{:S(2)}) copy-start(s32[512]{0:T(512)} %param.11) | copy-start | bytes 6148
  28.1 20.9 %all-to-all-start.1 = ((bf16[8,2,8,8,512]{4,2,3,1,0:T(8,128)(2,1)}), bf16[8,2,8,8,512]{4,2,3,1,0:T(8,128)(2,1)S(1)}, u32[]{:S(2)}, u32[]{:S(2)}) async-start(bf16[8,2,8,8,512]{4,2,3,1,0:T(8,128)(2,1)} %copy.27), calls=%async_computation.1 | async-start | bytes 2097152 | tf_op jit(solution)/shard_map/all_to_all | solution.py:31
  50.5 0.8 copy-start.1
  50.5 0.8 copy-start.2
where the time goes:
time: 240 us; the launch traced here: 239 us
  blocking collectives  63.8 us (27%)
  local copies, waits for them, and re-layouts  44.3 us (18%)
  matrix products  39.1 us (16%)
  waiting for transfers between devices  32.6 us (14%)
  loops' own time  30.1 us (13%)
  other arithmetic  17.7 us (7%)
  starting transfers between devices  11 us (5%)
    all_to_all x1, blocking collectives, exchange_both(): tiles = lax.all_to_all(tiles, axis, split_axis=0, concat_axis=0, tiled=True)  63.8 us
    all_to_all x2, waiting for transfers between devices, several_exchanges(): lax.all_to_all(section, axis, split_axis=0, concat_axis=0, tiled=True)  32.6 us
    another operation x1, loops' own time, body(): averaged = lax.map(one_channel, jnp.arange(chan_here, dtype=jnp.int32))  30.1 us
    dot_general x16, matrix products, channel_average(): jnp.dot(lower, onehot, preferred_element_type=jnp.float32)  19.2 us
    neg x16, other arithmetic, channel_average(): real_rows = jnp.concatenate([weights[0], -weights[1]], axis=0)  14.9 us
    squeeze x16, local copies, waits for them, and re-layouts, channel_average(): real_rows = jnp.concatenate([weights[0], -weights[1]], axis=0)  14.7 us
    dot_general x16, matrix products, channel_average(): jnp.dot(stacked_w.T, stacked_v, preferred_element_type=jnp.float32)  11.6 us
    all_to_all x2, starting transfers between devices, several_exchanges(): lax.all_to_all(section, axis, split_axis=0, concat_axis=0, tiled=True)  11 us
  transfers between devices with their start and end apart: 2, of which 2 were waited for; matrix products, arithmetic and copies ran while one was open for 1% of the time, Pallas kernels for 0%

commit v1 on v0

v1 whole, which is shorter than its diff:
```python
import functools

import jax
import jax.numpy as jnp
from jax import lax
from jax.experimental import pallas as pl
from jax.experimental.pallas import tpu as pltpu
from jax.sharding import PartitionSpec as P

TBINS = 64
CHUNKS = 1


def weight_rows_kernel(owners, weights_ref, rows_ref):
    per_owner = rows_ref.shape[1]
    span = rows_ref.shape[3]
    block = per_owner * span
    stacked = jnp.concatenate([weights_ref[0, 0], weights_ref[1, 0]], axis=0)
    new = lax.broadcasted_iota(jnp.int32, (block, block), 0)
    old = lax.broadcasted_iota(jnp.int32, (block, block), 1)
    wanted = (new % span) * per_owner + new // span
    pick = (wanted == old).astype(jnp.bfloat16)
    for at in range(owners):
        piece = stacked[:, at * block : (at + 1) * block]
        turned = lax.dot_general(
            pick, piece, (((1,), (1,)), ((), ())), preferred_element_type=jnp.float32
        ).astype(jnp.bfloat16)
        for j in range(per_owner):
            rows_ref[0, j, at] = turned[j * span : (j + 1) * span]


def weight_rows(weights, per_owner, dish_count, chan_count):
    _, chans, dishes, beams = weights.shape
    shape = (chans, per_owner, dish_count, chan_count, 2 * dishes)
    return pl.pallas_call(
        functools.partial(weight_rows_kernel, dish_count),
        grid=(chans,),
        in_specs=[pl.BlockSpec((2, 1, dishes, beams), lambda c: (0, c, 0, 0))],
        out_specs=pl.BlockSpec((1, *shape[1:]), lambda c: (c, 0, 0, 0, 0)),
        out_shape=jax.ShapeDtypeStruct(shape, jnp.bfloat16),
        cost_estimate=pl.CostEstimate(
            flops=2 * chans * beams * 128 * 2 * dishes,
            bytes_accessed=8 * chans * beams * dishes,
            transcendentals=0,
        ),
        name="weight_rows",
    )(weights)


def beam_kernel(samples, volts_ref, rows_ref, onehot_ref, inverse_ref, flag_ref, width_ref, out_ref):
    groups, _, _, inside, times = volts_ref.shape
    dishes = groups * inside
    real = volts_ref[:, 0, 0].reshape(dishes, times)
    imag = volts_ref[:, 0, 1].reshape(dishes, times)
    real_f, imag_f = real.astype(jnp.float32), imag.astype(jnp.float32)
    power = real_f * real_f + imag_f * imag_f
    first = jnp.sum(jnp.sum(power, axis=1, keepdims=True), axis=0, keepdims=True)
    second = jnp.sum(jnp.sum(power * power, axis=1, keepdims=True), axis=0, keepdims=True)
    mean_one = first / samples
    mean_two = second / samples
    ratio = mean_two / (mean_one * mean_one + 1e-06)
    kurtosis = (samples + 1.0) / (samples - 1.0) * (ratio - 1.0)
    excess = kurtosis - 1.0
    widths = width_ref[0]
    scaling = flag_ref[0] * widths / (widths + excess * excess)
    gain = (scaling * scaling) * inverse_ref[...]
    stacked = jnp.concatenate(
        [jnp.concatenate([real, imag], axis=1), jnp.concatenate([-imag, real], axis=1)], axis=0
    )
    summed = None
    for j in range(rows_ref.shape[1]):
        beams = jnp.dot(rows_ref[0, j], stacked, preferred_element_type=jnp.float32)
        re, im = beams[:, :times], beams[:, times:]
        detected = (re * re + im * im).astype(jnp.bfloat16)
        part = jnp.dot(detected, onehot_ref[j], preferred_element_type=jnp.float32)
        summed = part if summed is None else summed + part
    out_ref[0] = (summed * gain).astype(jnp.bfloat16)


def beam_power(samples, volts, rows, onehot, inverse, flag, width, first_chan):
    groups, chans, _, inside, times = volts.shape
    _, per_owner, owners, depth = rows.shape
    lanes = onehot.shape[2]
    whole = lambda *dims: pl.BlockSpec(dims, lambda c: (0,) * len(dims))
    return pl.pallas_call(
        functools.partial(beam_kernel, samples),
        grid=(chans,),
        in_specs=[
            pl.BlockSpec((groups, 1, 2, inside, times), lambda c: (0, c, 0, 0, 0)),
            pl.BlockSpec((1, per_owner, owners, depth), lambda c: (c + first_chan, 0, 0, 0)),
            whole(*onehot.shape),
            whole(*inverse.shape),
            pl.BlockSpec((1, 1, 1), lambda c: (c + first_chan, 0, 0)),
            pl.BlockSpec((1, 1, 1), lambda c: (c + first_chan, 0, 0)),
        ],
        out_specs=pl.BlockSpec((1, owners, lanes), lambda c: (c, 0, 0)),
        out_shape=jax.ShapeDtypeStruct((chans, owners, lanes), jnp.bfloat16),
        cost_estimate=pl.CostEstimate(
            flops=2 * chans * owners * per_owner * times * (2 * depth + lanes),
            bytes_accessed=2 * chans * (owners * per_owner * depth + depth * times + owners * lanes),
            transcendentals=0,
        ),
        name="beam_power",
    )(volts, rows, onehot, inverse, flag, width)


def body(voltages, beam_weights, flags, sk_bins, bin_of_sample):
    dish_count = lax.axis_size("dish")
    chan_count = lax.axis_size("chan")
    _, inside, chan_block, times = voltages.shape
    chans = chan_block // dish_count
    samples = float(inside * dish_count * times)
    owners = dish_count * chan_count
    per_owner = beam_weights.shape[3] // owners
    part = chans // CHUNKS

    by_peer = voltages.reshape(2, inside, dish_count, CHUNKS, part, times).transpose(3, 2, 4, 0, 1, 5)
    arrived = [
        lax.all_to_all(by_peer[k], "dish", split_axis=0, concat_axis=0, tiled=True)
        for k in range(CHUNKS)
    ]

    rows = weight_rows(beam_weights, per_owner, dish_count, chan_count)
    rows = rows.reshape(chans, per_owner, owners, -1)
    offset = lax.axis_index("dish") * chans
    flag = lax.dynamic_slice_in_dim(flags, offset, chans).astype(jnp.float32)
    width = 0.05 * lax.dynamic_slice_in_dim(sk_bins, offset, chans).astype(jnp.float32)
    matches = bin_of_sample[:, None] == jnp.arange(TBINS, dtype=jnp.int32)[None, :]
    inverse = jnp.tile(1.0 / jnp.sum(matches.astype(jnp.float32), axis=0), per_owner)[None, :]
    lane = jnp.arange(per_owner * TBINS, dtype=jnp.int32)
    place = jnp.arange(per_owner, dtype=jnp.int32)[:, None, None] * TBINS + bin_of_sample[None, :, None]
    onehot = (place == lane[None, None, :]).astype(jnp.bfloat16)

    moved = []
    for k in range(CHUNKS):
        power = beam_power(
            samples, arrived[k], rows, onehot, inverse, flag[:, None, None], width[:, None, None], k * part
        )
        blocks = power.reshape(part, dish_count, chan_count, -1).transpose(2, 1, 0, 3)
        blocks = blocks.reshape(owners, part, -1)
        moved.append(lax.all_to_all(blocks, ("chan", "dish"), split_axis=0, concat_axis=0, tiled=True))
    whole = jnp.concatenate(moved, axis=1)
    return whole.reshape(owners * chans, -1)


def solution(mesh):
    in_specs = (
        P(None, "dish", "chan", None),
        P(None, ("chan", "dish"), None, None),
        P("chan"),
        P("chan"),
        P(),
    )
    out_specs = P(None, ("dish", "chan"))
    return jax.shard_map(body, mesh=mesh, in_specs=in_specs, out_specs=out_specs, check_vma=False)
```

time: 240 us -> 134 us (0.56)
  matrix products: 39.1 us -> 0 us
  Pallas kernels: 0 us -> 33.1 us
  local copies, waits for them, and re-layouts: 44.3 us -> 11.5 us
  loops' own time: 30.1 us -> 0 us
  waiting for transfers between devices: 32.6 us -> 12.7 us
  other arithmetic: 17.7 us -> 1.69 us
  blocking collectives: 63.8 us -> 67.2 us
  starting transfers between devices: 11 us -> 7.6 us
    dot_general x48 -> x0, matrix products: 39.1 us -> none  [the longest x16 19.2 us: channel_average(): jnp.dot(lower, onehot, preferred_element_type=jnp.float32)]
    pallas_call x0 -> x2, Pallas kernels: none -> 33.1 us  [the longest x1 20.9 us: beam_power(): pl.pallas_call(functools.partial(beam_kernel, samples), grid=(chans,), in...]
    another operation x1 -> x0, loops' own time: 30.1 us -> none  [body(): averaged = lax.map(one_channel, jnp.arange(chan_here, dtype=jnp.int32))]
    all_to_all x2 -> x1, waiting for transfers between devices: 32.6 us -> 12.7 us  [body(): lax.all_to_all(by_peer[k], 'dish', split_axis=0, concat_axis=0, tiled=True)]
    squeeze x32 -> x0, local copies, waits for them, and re-layouts: 15 us -> none  [the longest x16 14.7 us: channel_average(): real_rows = jnp.concatenate([weights[0], -weights[1]], axis=0)]
    neg x16 -> x0, other arithmetic: 14.9 us -> none  [channel_average(): real_rows = jnp.concatenate([weights[0], -weights[1]], axis=0)]
    dynamic_slice x16 -> x0, local copies, waits for them, and re-layouts: 9.46 us -> none  [body(): averaged = lax.map(one_channel, jnp.arange(chan_here, dtype=jnp.int32))]
    unnamed x7 -> x10, local copies, waits for them, and re-layouts: 1.18 us -> 6.72 us
  transfers between devices with their start and end apart: 2 -> 1, of which waited for: 2 -> 1; matrix products, arithmetic and copies ran while one was open for 1% -> 3% of each run, Pallas kernels for 0% -> 9%
where the time goes in v1:
time: 134 us
  blocking collectives  67.2 us (50%)
  Pallas kernels  33.1 us (25%)
  waiting for transfers between devices  12.7 us (9%)
  local copies, waits for them, and re-layouts  11.5 us (9%)
  starting transfers between devices  7.6 us (6%)
  other arithmetic  1.69 us (1%)
    all_to_all x1, blocking collectives, body(): lax.all_to_all(blocks, ('chan', 'dish'), split_axis=0, concat_axis=0, til...  67.2 us
    pallas_call x1, Pallas kernels, beam_power(): pl.pallas_call(functools.partial(beam_kernel, samples), grid=(chans,), in...  20.9 us
    all_to_all x1, waiting for transfers between devices, body(): lax.all_to_all(by_peer[k], 'dish', split_axis=0, concat_axis=0, tiled=True)  12.7 us
    pallas_call x1, Pallas kernels, weight_rows(): pl.pallas_call(functools.partial(weight_rows_kernel, dish_count), grid=(c...  12.2 us
    all_to_all x1, starting transfers between devices, body(): lax.all_to_all(by_peer[k], 'dish', split_axis=0, concat_axis=0, tiled=True)  7.6 us
    unnamed x10, local copies, waits for them, and re-layouts  6.72 us
    reshape x1, local copies, waits for them, and re-layouts, body(): power.reshape(part, dish_count, chan_count, -1).transpose(2, 1, 0, 3)  2.76 us
  transfers between devices with their start and end apart: 1, of which 1 were waited for; matrix products, arithmetic and copies ran while one was open for 3% of the time, Pallas kernels for 9%

profile of v1, /device:TPU:1, one launch (start us, length us, event | category | flops | bytes accessed | tf_op | source)
XLA Modules:
  0.0 133.8 jit_solution(10154929456790936360)
XLA Ops:
  0.0 4.1 %copy.13 = bf16[2,8,128,512]{3,1,0,2:T(8,128)(2,1)} copy(bf16[2,8,128,512]{3,2,1,0:T(8,128)(2,1)} %param.5) | data formatting | bytes 4194304 | tf_op args[0]
  4.1 0.0 copy-start.1
  4.1 0.0 copy-start.2
  4.1 0.0 copy-start.3
  4.1 7.6 %all-to-all-start = ((bf16[8,16,2,8,512]{4,3,2,1,0:T(8,128)(2,1)}), bf16[8,16,2,8,512]{4,3,2,1,0:T(8,128)(2,1)S(1)}, u32[]{:S(2)}, u32[]{:S(2)}) async-start(bf16[8,16,2,8,512]{4,3,2,1,0:T(8,128)(2,1)} %bitcast.2), calls=%async_computation | async-start | bytes 4194304 | tf_op jit(solution)/shard_map/all_to_all | solution.py:119
  11.7 0.0 copy-done.1
  11.7 0.1 convert_reduce_fusion
  11.8 0.7 broadcast_in_dim_tile.3.inverse_ref
  12.5 0.0 copy-done.2
  12.5 0.1 multiply_bitcast_fusion
  12.5 0.7 copy.15.width_ref
  13.2 0.0 copy-done.3
  13.2 0.1 convert_bitcast_fusion
  13.3 0.7 copy.14.flag_ref
  14.0 12.2 %weight_rows.1 = bf16[16,4,8,32,128]{4,3,2,1,0:T(8,128)(2,1)} custom-call(bf16[2,16,64,1024]{3,2,1,0:T(8,128)(2,1)} %weights_ref.1), custom_call_target="tpu_custom_call" | custom-call | flops 536870912 | bytes 8388608 | tf_op jit(solution)/shard_map/weight_rows/pallas_call | solution.py:35
  26.1 0.1 broadcast_add_fusion
  26.2 1.3 %fusion.onehot_ref = bf16[4,512,256]{2,1,0:T(8,128)(2,1)} fusion(s32[4,512]{1,0:T(4,128)S(1)} %broadcast_add_fusion), kind=kLoop, calls=%fused_computation.1 | loop fusion | flops 1048576 | bytes 1056768 | tf_op jit(solution)/shard_map/convert_element_type | solution.py:132
  27.6 12.7 %all-to-all-done.volts_ref = bf16[8,16,2,8,512]{4,3,2,1,0:T(8,128)(2,1)S(1)} async-done(((bf16[8,16,2,8,512]{4,3,2,1,0:T(8,128)(2,1)}), bf16[8,16,2,8,512]{4,3,2,1,0:T(8,128)(2,1)S(1)}, u32[]{:S(2)}, u32[]{:S(2)}) %all-to-all-start) | async-done | bytes 2097184 | tf_op jit(solution)/shard_map/all_to_all | solution.py:119
  40.3 0.0 copy-start
  40.3 1.3 copy-done
  41.6 20.9 %beam_power.1 = bf16[16,256,256]{2,1,0:T(8,128)(2,1)} custom-call(bf16[8,16,2,8,512]{4,3,2,1,0:T(8,128)(2,1)} %copy-done, bf16[16,4,256,128]{3,2,1,0:T(8,128)(2,1)} %bitcast.17, bf16[4,512,256]{2,1,0:T(8,128)(2,1)} %fusion.onehot_ref, f32[1,256]{1,0:T(1,128)} %broadcast_in_dim_tile.3.inverse_ref, f32[16,1,1]{2,1,0:T(1,128)} %copy.14.flag_ref, ...), custom_call_target="tpu_custom_call" | custom-call | flops 8589934592 | bytes 8388608 | tf_op jit(solution)/shard_map/beam_power/pallas_call | solution.py:85
  62.5 2.8 %copy.16 = bf16[16,8,32,256]{3,0,1,2:T(8,128)(2,1)S(1)} copy(bf16[16,8,32,256]{3,2,1,0:T(8,128)(2,1)} %bitcast.18) | data formatting | bytes 4194304 | tf_op jit(solution)/shard_map/reshape | solution.py:139
  65.3 67.2 %all_to_all.10 = bf16[256,16,256]{2,1,0:T(8,128)(2,1)S(1)} all-to-all(bf16[256,16,256]{2,1,0:T(8,128)(2,1)S(1)} %bitcast.15), channel_id=1, replica_groups=mesh['dish'=8,'chan'=32] {'chan','dish'}, dimensions={0} | all-to-all | bytes 4194304 | tf_op jit(solution)/shard_map/all_to_all | solution.py:141
  132.5 1.3 copy.18
  (3 shorter events, 0.0 us)
Async XLA Ops:
  4.1 7.6 %copy-start.1 = (s32[512]{0:T(512)S(1)}, s32[512]{0:T(512)}, u32[]{:S(2)}) copy-start(s32[512]{0:T(512)} %param.9) | copy-start | bytes 6148
  4.1 8.4 %copy-start.2 = (s32[128]{0:T(128)S(1)}, s32[128]{0:T(128)}, u32[]{:S(2)}) copy-start(s32[128]{0:T(128)} %param.8) | copy-start | bytes 1540
  4.1 9.1 %copy-start.3 = (s32[128]{0:T(128)S(1)}, s32[128]{0:T(128)}, u32[]{:S(2)}) copy-start(s32[128]{0:T(128)} %param.7) | copy-start | bytes 1540
  4.1 36.2 %all-to-all-start = ((bf16[8,16,2,8,512]{4,3,2,1,0:T(8,128)(2,1)}), bf16[8,16,2,8,512]{4,3,2,1,0:T(8,128)(2,1)S(1)}, u32[]{:S(2)}, u32[]{:S(2)}) async-start(bf16[8,16,2,8,512]{4,3,2,1,0:T(8,128)(2,1)} %bitcast.2), calls=%async_computation | async-start | bytes 4194304 | tf_op jit(solution)/shard_map/all_to_all | solution.py:119
  40.3 1.3 copy-start

commit v2 on v1

v2 whole, which is shorter than its diff:
```python
import functools

import jax
import jax.numpy as jnp
from jax import lax
from jax.experimental import pallas as pl
from jax.experimental.pallas import tpu as pltpu
from jax.sharding import PartitionSpec as P

TBINS = 64
STEP = 4
ROW = 4
VMEM_LIMIT = 46 * 1024 * 1024


def member(place, count):
    return place % (count // ROW) * ROW + place // (count // ROW)


def weight_rows_kernel(owners, weights_ref, rows_ref):
    per_owner = rows_ref.shape[1]
    span = rows_ref.shape[3]
    block = per_owner * span
    inside = weights_ref.shape[2] // owners
    stacked = []
    for part in range(2):
        for place in range(owners):
            start = member(place, owners) * inside
            stacked.append(weights_ref[part, 0, start : start + inside, :])
    stacked = jnp.concatenate(stacked, axis=0)
    new = lax.broadcasted_iota(jnp.int32, (block, block), 0)
    old = lax.broadcasted_iota(jnp.int32, (block, block), 1)
    wanted = (new % span) * per_owner + new // span
    pick = (wanted == old).astype(jnp.bfloat16)
    for at in range(owners):
        piece = stacked[:, at * block : (at + 1) * block]
        turned = lax.dot_general(
            pick, piece, (((1,), (1,)), ((), ())), preferred_element_type=jnp.float32
        ).astype(jnp.bfloat16)
        for j in range(per_owner):
            rows_ref[0, j, at] = turned[j * span : (j + 1) * span]


def weight_rows(weights, per_owner, dish_count, chan_count):
    _, chans, dishes, beams = weights.shape
    shape = (chans, per_owner, dish_count, chan_count, 2 * dishes)
    return pl.pallas_call(
        functools.partial(weight_rows_kernel, dish_count),
        grid=(chans,),
        in_specs=[pl.BlockSpec((2, 1, dishes, beams), lambda c: (0, c, 0, 0))],
        out_specs=pl.BlockSpec((1, *shape[1:]), lambda c: (c, 0, 0, 0, 0)),
        out_shape=jax.ShapeDtypeStruct(shape, jnp.bfloat16),
        compiler_params=pltpu.CompilerParams(vmem_limit_bytes=VMEM_LIMIT),
        cost_estimate=pl.CostEstimate(
            flops=2 * chans * beams * 128 * 2 * dishes,
            bytes_accessed=8 * chans * beams * dishes,
            transcendentals=0,
        ),
        name="weight_rows",
    )(weights)


def channel_power(samples, at, volts_ref, rows_ref, onehot_ref, inverse_ref, flag_ref, width_ref):
    groups, _, _, inside, times = volts_ref.shape
    dishes = groups * inside
    real = volts_ref[:, at, 0].reshape(dishes, times)
    imag = volts_ref[:, at, 1].reshape(dishes, times)
    real_f, imag_f = real.astype(jnp.float32), imag.astype(jnp.float32)
    power = real_f * real_f + imag_f * imag_f
    first = jnp.sum(jnp.sum(power, axis=1, keepdims=True), axis=0, keepdims=True)
    second = jnp.sum(jnp.sum(power * power, axis=1, keepdims=True), axis=0, keepdims=True)
    mean_one = first / samples
    mean_two = second / samples
    ratio = mean_two / (mean_one * mean_one + 1e-06)
    kurtosis = (samples + 1.0) / (samples - 1.0) * (ratio - 1.0)
    excess = kurtosis - 1.0
    widths = width_ref[at]
    scaling = flag_ref[at] * widths / (widths + excess * excess)
    gain = (scaling * scaling) * inverse_ref[...]
    stacked = jnp.concatenate(
        [jnp.concatenate([real, imag], axis=1), jnp.concatenate([-imag, real], axis=1)], axis=0
    )
    detected = []
    for j in range(rows_ref.shape[1]):
        beams = jnp.dot(rows_ref[at, j], stacked, preferred_element_type=jnp.float32)
        re, im = beams[:, :times], beams[:, times:]
        detected.append((re * re + im * im).astype(jnp.bfloat16))
    summed = jnp.dot(
        jnp.concatenate(detected, axis=1), onehot_ref[...], preferred_element_type=jnp.float32
    )
    return summed * gain


def beam_kernel(samples, *refs):
    *operands, out_ref = refs
    for at in range(STEP):
        out_ref[at] = channel_power(samples, at, *operands).astype(jnp.bfloat16)


def beam_power(samples, volts, rows, onehot, inverse, flag, width):
    groups, chans, _, inside, times = volts.shape
    _, per_owner, owners, depth = rows.shape
    lanes = onehot.shape[1]
    whole = lambda *dims: pl.BlockSpec(dims, lambda c: (0,) * len(dims))
    return pl.pallas_call(
        functools.partial(beam_kernel, samples),
        grid=(chans // STEP,),
        in_specs=[
            pl.BlockSpec((groups, STEP, 2, inside, times), lambda c: (0, c, 0, 0, 0)),
            pl.BlockSpec((STEP, per_owner, owners, depth), lambda c: (c, 0, 0, 0)),
            whole(*onehot.shape),
            whole(*inverse.shape),
            pl.BlockSpec((STEP, 1, 1), lambda c: (c, 0, 0)),
            pl.BlockSpec((STEP, 1, 1), lambda c: (c, 0, 0)),
        ],
        out_specs=pl.BlockSpec((STEP, owners, lanes), lambda c: (c, 0, 0)),
        out_shape=jax.ShapeDtypeStruct((chans, owners, lanes), jnp.bfloat16),
        compiler_params=pltpu.CompilerParams(vmem_limit_bytes=VMEM_LIMIT),
        cost_estimate=pl.CostEstimate(
            flops=2 * chans * owners * per_owner * times * (2 * depth + lanes),
            bytes_accessed=2 * chans * (owners * per_owner * depth + depth * times + owners * lanes),
            transcendentals=0,
        ),
        name="beam_power",
    )(volts, rows, onehot, inverse, flag, width)


def body(voltages, beam_weights, flags, sk_bins, bin_of_sample):
    dish_count = lax.axis_size("dish")
    chan_count = lax.axis_size("chan")
    _, inside, chan_block, times = voltages.shape
    chans = chan_block // dish_count
    samples = float(inside * dish_count * times)
    owners = dish_count * chan_count
    per_owner = beam_weights.shape[3] // owners

    by_peer = voltages.reshape(2, inside, dish_count // ROW, ROW, chans, times)
    arrived = lax.all_to_all(
        by_peer.transpose(3, 2, 4, 0, 1, 5).reshape(dish_count, chans, 2, inside, times),
        "dish",
        split_axis=0,
        concat_axis=0,
        tiled=True,
        axis_index_groups=[[member(i, dish_count) for i in range(dish_count)]],
    )

    rows = weight_rows(beam_weights, per_owner, dish_count, chan_count)
    rows = rows.reshape(chans, per_owner, owners, -1)
    offset = lax.axis_index("dish") * chans
    flag = lax.dynamic_slice_in_dim(flags, offset, chans).astype(jnp.float32)
    width = 0.05 * lax.dynamic_slice_in_dim(sk_bins, offset, chans).astype(jnp.float32)
    matches = bin_of_sample[:, None] == jnp.arange(TBINS, dtype=jnp.int32)[None, :]
    inverse = jnp.tile(1.0 / jnp.sum(matches.astype(jnp.float32), axis=0), per_owner)[None, :]
    lane = jnp.arange(per_owner * TBINS, dtype=jnp.int32)
    place = jnp.arange(per_owner, dtype=jnp.int32)[:, None, None] * TBINS + bin_of_sample[None, :, None]
    onehot = (place == lane[None, None, :]).astype(jnp.bfloat16).reshape(per_owner * times, -1)

    power = beam_power(
        samples, arrived, rows, onehot, inverse, flag[:, None, None], width[:, None, None]
    )
    blocks = power.reshape(chans, dish_count, chan_count, -1).transpose(2, 1, 0, 3)
    moved = lax.all_to_all(
        blocks.reshape(owners, chans, -1), ("chan", "dish"), split_axis=0, concat_axis=0, tiled=True
    )
    return moved.reshape(owners * chans, -1)


def solution(mesh):
    in_specs = (
        P(None, "dish", "chan", None),
        P(None, ("chan", "dish"), None, None),
        P("chan"),
        P("chan"),
        P(),
    )
    out_specs = P(None, ("dish", "chan"))
    return jax.shard_map(body, mesh=mesh, in_specs=in_specs, out_specs=out_specs, check_vma=False)
```

time: 134 us -> 126 us (0.940)
  Pallas kernels: 33.1 us -> 26.4 us
  waiting for transfers between devices: 12.7 us -> 17.1 us
  local copies, waits for them, and re-layouts: 11.5 us -> 8.93 us
  blocking collectives: 67.2 us -> 64.9 us
    pallas_call x1, Pallas kernels: 20.9 us -> 15.9 us  [beam_power(): pl.pallas_call(functools.partial(beam_kernel, samples), grid=(chans // ST...]
    all_to_all x1, waiting for transfers between devices: 12.7 us -> 17.1 us  [body(): lax.all_to_all(by_peer.transpose(3, 2, 4, 0, 1, 5).reshape(dish_count, ch...]
    unnamed x10 -> x11, local copies, waits for them, and re-layouts: 6.72 us -> 3.34 us
    reshape x1 -> x2, local copies, waits for them, and re-layouts: 2.76 us -> 5.32 us  [the longest x1 4.14 us: body(): by_peer = voltages.reshape(2, inside, dish_count // ROW, ROW, chans, times)]
    all_to_all x1, blocking collectives: 67.2 us -> 64.9 us  [body(): lax.all_to_all(blocks.reshape(owners, chans, -1), ('chan', 'dish'), split...]
    pallas_call x1, Pallas kernels: 12.2 us -> 10.5 us  [weight_rows(): pl.pallas_call(functools.partial(weight_rows_kernel, dish_count), grid=(c...]
  transfers between devices with their start and end apart: 1 -> 1, of which waited for: 1 -> 1; matrix products, arithmetic and copies ran while one was open for 3% -> 1% of each run, Pallas kernels for 9% -> 8%
where the time goes in v2:
time: 126 us
  blocking collectives  64.9 us (52%)
  Pallas kernels  26.4 us (21%)
  waiting for transfers between devices  17.1 us (14%)
  local copies, waits for them, and re-layouts  8.93 us (7%)
  starting transfers between devices  7.6 us (6%)
    all_to_all x1, blocking collectives, body(): lax.all_to_all(blocks.reshape(owners, chans, -1), ('chan', 'dish'), split...  64.9 us
    all_to_all x1, waiting for transfers between devices, body(): lax.all_to_all(by_peer.transpose(3, 2, 4, 0, 1, 5).reshape(dish_count, ch...  17.1 us
    pallas_call x1, Pallas kernels, beam_power(): pl.pallas_call(functools.partial(beam_kernel, samples), grid=(chans // ST...  15.9 us
    pallas_call x1, Pallas kernels, weight_rows(): pl.pallas_call(functools.partial(weight_rows_kernel, dish_count), grid=(c...  10.5 us
    all_to_all x1, starting transfers between devices, body(): lax.all_to_all(by_peer.transpose(3, 2, 4, 0, 1, 5).reshape(dish_count, ch...  7.6 us
    reshape x1, local copies, waits for them, and re-layouts, body(): by_peer = voltages.reshape(2, inside, dish_count // ROW, ROW, chans, times)  4.14 us
    unnamed x11, local copies, waits for them, and re-layouts  3.34 us
  transfers between devices with their start and end apart: 1, of which 1 were waited for; matrix products, arithmetic and copies ran while one was open for 1% of the time, Pallas kernels for 8%

profile of v2, /device:TPU:1, one launch (start us, length us, event | category | flops | bytes accessed | tf_op | source)
XLA Modules:
  0.0 125.7 jit_solution(2900727862888833224)
XLA Ops:
  0.0 4.1 %copy.13 = bf16[2,8,2,4,16,512]{5,1,0,4,2,3:T(8,128)(2,1)} copy(bf16[2,8,2,4,16,512]{5,4,3,2,1,0:T(8,128)(2,1)} %bitcast.23) | data formatting | bytes 4194304 | tf_op jit(solution)/shard_map/reshape | solution.py:137
  4.1 0.0 copy-start.1
  4.1 0.0 copy-start.2
  4.2 0.0 copy-start.3
  4.2 7.6 %all-to-all-start = ((bf16[8,16,2,8,512]{4,3,2,1,0:T(8,128)(2,1)}), bf16[8,16,2,8,512]{4,3,2,1,0:T(8,128)(2,1)S(1)}, u32[]{:S(2)}, u32[]{:S(2)}) async-start(bf16[8,16,2,8,512]{4,3,2,1,0:T(8,128)(2,1)} %bitcast.20), calls=%async_computation | async-start | bytes 4194304 | tf_op jit(solution)/shard_map/all_to_all | solution.py:138
  11.8 0.0 copy-done.1
  11.8 0.1 convert_reduce_fusion
  11.9 0.1 broadcast_in_dim_tile.3.refs_3_
  12.0 0.1 broadcast_bitcast_fusion
  12.1 0.0 copy-done.2
  12.1 0.1 multiply_bitcast_fusion
  12.1 0.1 copy.15.refs_5_
  12.2 0.0 copy-done.3
  12.2 0.1 convert_bitcast_fusion
  12.3 0.1 copy.14.refs_4_
  12.4 10.5 %weight_rows.1 = bf16[16,4,8,32,128]{4,3,2,1,0:T(8,128)(2,1)S(1)} custom-call(bf16[2,16,64,1024]{3,2,1,0:T(8,128)(2,1)} %weights_ref.1), custom_call_target="tpu_custom_call" | custom-call | flops 536870912 | bytes 8388608 | tf_op jit(solution)/shard_map/weight_rows/pallas_call | solution.py:47
  23.0 0.0 copy-start
  23.0 1.9 %copy-done = bf16[16,4,8,32,128]{4,3,2,1,0:T(8,128)(2,1)} copy-done((bf16[16,4,8,32,128]{4,3,2,1,0:T(8,128)(2,1)}, bf16[16,4,8,32,128]{4,3,2,1,0:T(8,128)(2,1)S(1)}, u32[]{:S(2)}) %copy-start) | copy-done | bytes 4194328
  24.9 0.3 fusion.refs_2_
  25.2 17.1 %all-to-all-done.refs_0_ = bf16[8,16,2,8,512]{4,3,2,1,0:T(8,128)(2,1)S(1)} async-done(((bf16[8,16,2,8,512]{4,3,2,1,0:T(8,128)(2,1)}), bf16[8,16,2,8,512]{4,3,2,1,0:T(8,128)(2,1)S(1)}, u32[]{:S(2)}, u32[]{:S(2)}) %all-to-all-start) | async-done | bytes 2097184 | tf_op jit(solution)/shard_map/all_to_all | solution.py:138
  42.4 15.9 %beam_power.1 = bf16[16,256,256]{2,1,0:T(8,128)(2,1)S(1)} custom-call(bf16[8,16,2,8,512]{4,3,2,1,0:T(8,128)(2,1)S(1)} %all-to-all-done.refs_0_, bf16[16,4,256,128]{3,2,1,0:T(8,128)(2,1)} %bitcast.18, bf16[2048,256]{1,0:T(8,128)(2,1)S(1)} %fusion.refs_2_, f32[1,256]{1,0:T(1,128)S(1)} %broadcast_in_dim_tile.3.refs_3_, f32[16,1,1]{2,1,0:T(1,128)S(1)} %copy.14.refs_4_, ...), custom_call_target="tpu_custom_call" | custom-call | flops 8589934592 | bytes 8388608 | tf_op jit(solution)/shard_map/beam_power/pallas_call | solution.py:105
  58.2 1.2 copy.16
  59.4 64.9 %all_to_all.10 = bf16[256,16,256]{2,1,0:T(8,128)(2,1)S(1)} all-to-all(bf16[256,16,256]{2,1,0:T(8,128)(2,1)S(1)} %bitcast.21), channel_id=1, replica_groups=mesh['dish'=8,'chan'=32] {'chan','dish'}, dimensions={0} | all-to-all | bytes 4194304 | tf_op jit(solution)/shard_map/all_to_all | solution.py:162
  124.4 1.3 %copy.19 = bf16[4096,256]{1,0:T(8,128)(2,1)} copy(bf16[4096,256]{1,0:T(8,128)(2,1)S(1)} %bitcast.22) | data formatting | bytes 4194304
  (6 shorter events, 0.0 us)
Async XLA Ops:
  4.1 7.6 %copy-start.1 = (s32[512]{0:T(512)S(1)}, s32[512]{0:T(512)}, u32[]{:S(2)}) copy-start(s32[512]{0:T(512)} %param.9) | copy-start | bytes 6148
  4.1 7.9 %copy-start.2 = (s32[128]{0:T(128)S(1)}, s32[128]{0:T(128)}, u32[]{:S(2)}) copy-start(s32[128]{0:T(128)} %param.8) | copy-start | bytes 1540
  4.2 8.1 %copy-start.3 = (s32[128]{0:T(128)S(1)}, s32[128]{0:T(128)}, u32[]{:S(2)}) copy-start(s32[128]{0:T(128)} %param.7) | copy-start | bytes 1540
  4.2 38.2 %all-to-all-start = ((bf16[8,16,2,8,512]{4,3,2,1,0:T(8,128)(2,1)}), bf16[8,16,2,8,512]{4,3,2,1,0:T(8,128)(2,1)S(1)}, u32[]{:S(2)}, u32[]{:S(2)}) async-start(bf16[8,16,2,8,512]{4,3,2,1,0:T(8,128)(2,1)} %bitcast.20), calls=%async_computation | async-start | bytes 4194304 | tf_op jit(solution)/shard_map/all_to_all | solution.py:138
  23.0 1.9 %copy-start = (bf16[16,4,8,32,128]{4,3,2,1,0:T(8,128)(2,1)}, bf16[16,4,8,32,128]{4,3,2,1,0:T(8,128)(2,1)S(1)}, u32[]{:S(2)}) copy-start(bf16[16,4,8,32,128]{4,3,2,1,0:T(8,128)(2,1)S(1)} %weight_rows.1) | copy-start | bytes 12582916
